TPU v7x, 32 devices: a whole 2x2x4 slice. The times are simulated.
32 devices in a mesh: groups: 2 (over y), seq: 4 (over z), head: 2 (over x), inner: 2 (over core).
Axes of the slice: x: 2, y: 2, z: 4, core: 2. Of those that a mesh axis runs over, the one named last changes fastest.
Arguments:
- queries: bfloat16 [4096, 2, 8, 128], P(('groups', 'seq'), 'head', 'inner'), parts along dimension 0, may hold values from -120 to 120
- grad_out: bfloat16 [4096, 2, 8, 128], P(('groups', 'seq'), 'head', 'inner'), parts along dimension 0, may hold values from -6 to 6
- keys: bfloat16 [4096, 2, 128], P(('groups', 'seq'), 'head'), parts along dimension 0, may hold values from -6 to 6
- values: bfloat16 [4096, 2, 128], P(('groups', 'seq'), 'head'), parts along dimension 0, may hold values from -6 to 6
- indices: int32 [2, 64, 16], P('head', 'groups'), parts along dimension 1, may hold values from 0 to 31, as said below
- valid: int32 [2, 64, 16], P('head', 'groups'), parts along dimension 1, may hold values from 0 to 1
Outputs:
- grad_queries: bfloat16 [4096, 2, 8, 128], P(('groups', 'seq'), 'head', 'inner'), parts along dimension 0
- grad_keys: bfloat16 [4096, 2, 128], P(('groups', 'seq'), 'head'), parts along dimension 0
- grad_values: bfloat16 [4096, 2, 128], P(('groups', 'seq'), 'head'), parts along dimension 0
There are 2 independent parts, one for each index of `groups`. A program takes and returns all parts, laid end to end along the dimension named above; each array names one. Nothing has to cross between parts.
Inputs may be any that keep to these rules, and one draw needn't show every extreme that they name: `indices`: call blocks r * 8 to r * 8 + 7 run r. For every KV head and query block b: slot 0 names b and is valid; the valid slots name distinct blocks at most b; over all query blocks of run r, the valid slots name blocks of runs later than r never, and for each earlier run exactly 4 distinct blocks of it. Slots that are not valid name arbitrary blocks.
All inputs are finite; a program needn't handle non-finite values.
Results may differ from a plain program's by a relative error of at most 0.007.
Values may be sent and summed in bfloat16 or wider, within the bound.
No kernel may reach another device: no remote copies, remote signals or barrier semaphores. Data moves between devices by JAX's collectives and lax.ppermute only.
A program may use at most 64 MiB of HBM per device.

v0:
```python
import math
import jax
import jax.numpy as jnp
from jax import lax
from jax.sharding import PartitionSpec as P

BLK = 64
TOPK = 16
CAP = 4


def per_device(queries, grad_out, keys, values, indices, valid):
    tokens = queries.shape[0]
    heads_here = queries.shape[2]
    width = queries.shape[3]
    seq_count = lax.axis_size("seq")
    seq_here = lax.axis_index("seq")
    blocks_here = tokens // BLK
    total_blocks = indices.shape[1]
    scaling = 1.0 / math.sqrt(width)
    remote_rows = seq_count * CAP
    dest_rows = remote_rows + blocks_here
    picks_all = indices[0]
    valid_all = valid[0] > 0
    owner_all = picks_all // blocks_here
    local_all = picks_all % blocks_here
    my_picks = lax.dynamic_slice_in_dim(picks_all, seq_here * blocks_here, blocks_here, 0)
    my_valid = lax.dynamic_slice_in_dim(valid_all, seq_here * blocks_here, blocks_here, 0)
    my_owner = my_picks // blocks_here
    my_local = my_picks % blocks_here
    remote = my_valid & (my_owner != seq_here)
    block_ids = jnp.arange(total_blocks, dtype=jnp.int32)
    hits_in = (my_picks[:, :, None] == block_ids[None, None, :]) & remote[:, :, None]
    present_in = jnp.any(hits_in, axis=(0, 1)).reshape(seq_count, blocks_here)
    rank_in = jnp.cumsum(present_in.astype(jnp.int32), axis=1) - 1
    slot_ref = jnp.sum(jnp.where(hits_in, rank_in.reshape(-1)[None, None, :], 0), axis=2)
    row_index = jnp.where(remote, my_owner * CAP + slot_ref, remote_rows + my_local)
    source_run = block_ids // blocks_here
    incoming = valid_all & (owner_all == seq_here) & (source_run != seq_here)[:, None]
    hits_out = (
        local_all[:, :, None] == jnp.arange(blocks_here, dtype=jnp.int32)[None, None, :]
    ) & incoming[:, :, None]
    present_out = jnp.any(hits_out.reshape(seq_count, blocks_here * TOPK, blocks_here), axis=1)
    rank_out = jnp.cumsum(present_out.astype(jnp.int32), axis=1) - 1
    choose_out = present_out[:, None, :] & (
        rank_out[:, None, :] == jnp.arange(CAP, dtype=jnp.int32)[None, :, None]
    )
    wanted = my_picks.reshape(-1)
    blank = jnp.zeros((blocks_here * TOPK, BLK, width), jnp.bfloat16)
    carry = (blank, blank)
    key_piece = lax.all_gather(keys, "seq", axis=0, tiled=True)
    value_piece = lax.all_gather(values, "seq", axis=0, tiled=True)
    count = key_piece.shape[0] // BLK
    relative = wanted
    inside = (relative >= 0) & (relative < count)
    relative = jnp.clip(relative, 0, count - 1)
    key_rows = jnp.take(key_piece[:, 0].reshape(count, BLK, width), relative, axis=0)
    value_rows = jnp.take(value_piece[:, 0].reshape(count, BLK, width), relative, axis=0)
    sel_keys = jnp.where(inside[:, None, None], key_rows, carry[0])
    sel_values = jnp.where(inside[:, None, None], value_rows, carry[1])
    group = math.gcd(blocks_here, max(1, 512 // (BLK * heads_here)))
    steps_count = blocks_here // group
    span = TOPK * BLK
    position = jnp.arange(BLK, dtype=jnp.int32)
    causal = position[None, :] <= position[:, None]
    block_global = seq_here * blocks_here + jnp.arange(blocks_here, dtype=jnp.int32)
    before = my_picks < block_global[:, None]
    same = my_picks == block_global[:, None]
    allowed = my_valid[:, None, :, None] & (
        before[:, None, :, None] | same[:, None, :, None] & causal[None, :, None, :]
    )
    allowed = allowed.reshape(steps_count, group, BLK, span)
    query_steps = queries[:, 0].reshape(steps_count, group, BLK, heads_here, width)
    grad_steps = grad_out[:, 0].reshape(steps_count, group, BLK, heads_here, width)
    key_steps = sel_keys.reshape(steps_count, group, span, width)
    value_steps = sel_values.reshape(steps_count, group, span, width)
    row_steps = row_index.reshape(steps_count, group * TOPK)

    def attend(carry, inputs):
        key_acc, value_acc = carry
        q_group, do_group, k_group, v_group, mask_group, rows_group = inputs
        mask_heads = mask_group[:, None, :, :]
        scores = (
            jnp.einsum("qigw,qsw->qgis", q_group, k_group, preferred_element_type=jnp.float32)
            * scaling
        )
        highest = jnp.max(jnp.where(mask_heads, scores, -jnp.inf), axis=-1, keepdims=True)
        weights = jnp.where(mask_heads, jnp.exp(scores - highest), 0.0)
        probs = weights / jnp.sum(weights, axis=-1, keepdims=True)
        probs_b = probs.astype(jnp.bfloat16)
        dprobs = jnp.einsum("qigw,qsw->qgis", do_group, v_group, preferred_element_type=jnp.float32)
        delta = jnp.sum(probs * dprobs, axis=-1, keepdims=True)
        dscores = (probs * (dprobs - delta)).astype(jnp.bfloat16)
        query_grad = (
            jnp.einsum("qgis,qsw->qigw", dscores, k_group, preferred_element_type=jnp.float32)
            * scaling
        ).astype(jnp.bfloat16)
        key_terms = (
            jnp.einsum("qgis,qigw->qsw", dscores, q_group, preferred_element_type=jnp.float32)
            * scaling
        )
        value_terms = jnp.einsum(
            "qgis,qigw->qsw", probs_b, do_group, preferred_element_type=jnp.float32
        )
        key_acc = key_acc.at[rows_group].add(key_terms.reshape(group * TOPK, BLK * width))
        value_acc = value_acc.at[rows_group].add(value_terms.reshape(group * TOPK, BLK * width))
        return ((key_acc, value_acc), query_grad)

    zeros_dest = jnp.zeros((dest_rows, BLK * width), jnp.float32)
    (key_acc, value_acc), query_grads = lax.scan(
        attend,
        (zeros_dest, zeros_dest),
        (query_steps, grad_steps, key_steps, value_steps, allowed, row_steps),
    )
    grad_queries = query_grads.reshape(tokens, 1, heads_here, width)
    send_key_tiles = key_acc[:remote_rows].reshape(seq_count, CAP, BLK * width)
    send_value_tiles = value_acc[:remote_rows].reshape(seq_count, CAP, BLK * width)
    own_keys = key_acc[remote_rows:]
    own_values = value_acc[remote_rows:]
    choose_float = choose_out.astype(jnp.float32)
    back_keys, back_values = (
        lax.all_to_all(send_key_tiles, "seq", split_axis=0, concat_axis=0, tiled=True),
        lax.all_to_all(send_value_tiles, "seq", split_axis=0, concat_axis=0, tiled=True),
    )
    local_keys = own_keys + jnp.einsum(
        "dcb,dcx->bx", choose_float, back_keys, precision=lax.Precision.HIGHEST
    )
    local_values = own_values + jnp.einsum(
        "dcb,dcx->bx", choose_float, back_values, precision=lax.Precision.HIGHEST
    )
    total_keys, total_values = lax.psum((local_keys, local_values), "inner")
    grad_keys = total_keys.astype(jnp.bfloat16).reshape(tokens, 1, width)
    grad_values = total_values.astype(jnp.bfloat16).reshape(tokens, 1, width)
    return (grad_queries, grad_keys, grad_values)


def solution(mesh):
    return jax.shard_map(
        per_device,
        mesh=mesh,
        in_specs=(
            P(("groups", "seq"), "head", "inner", None),
            P(("groups", "seq"), "head", "inner", None),
            P(("groups", "seq"), "head", None),
            P(("groups", "seq"), "head", None),
            P("head", "groups", None),
            P("head", "groups", None),
        ),
        out_specs=(
            P(("groups", "seq"), "head", "inner", None),
            P(("groups", "seq"), "head", None),
            P(("groups", "seq"), "head", None),
        ),
        check_vma=False,
    )
```

profile of v0, /device:TPU:0, one launch (start us, length us, event | category | flops | bytes accessed | tf_op | source)
XLA Modules:
  0.0 166.9 jit_solution(11409170172867323838)
XLA Ops:
  4.3 17.6 %all_gather.6 = bf16[2048,1,128]{2,0,1:T(8,128)(2,1)S(1)} all-gather(bf16[512,1,128]{2,0,1:T(8,128)(2,1)} %param.12), channel_id=1, replica_groups=mesh['groups'=2,'seq'=4,'head'=2,'inner'=2] {'seq'}, dimensions={0}, use_global_device_ids=true | all-gather | bytes 655360 | tf_op jit(solution)/shard_map/all_gather | solution.py:51
  21.9 16.6 %all_gather.7 = bf16[2048,1,128]{2,0,1:T(8,128)(2,1)S(1)} all-gather(bf16[512,1,128]{2,0,1:T(8,128)(2,1)} %param.13), channel_id=1, replica_groups=mesh['groups'=2,'seq'=4,'head'=2,'inner'=2] {'seq'}, dimensions={0}, use_global_device_ids=true | all-gather | bytes 655360 | tf_op jit(solution)/shard_map/all_gather | solution.py:52
  38.5 1.0 gather_fusion.1
  39.4 2.1 %gather_fusion = bf16[128,64,128]{2,1,0:T(8,128)(2,1)} fusion(bf16[32,64,128]{2,1,0:T(8,128)(2,1)S(1)} %bitcast.131, s32[1024]{0:T(1024)S(1)} %pad_clamp_fusion), kind=kCustom, calls=%fused_computation.clone | custom fusion | bytes 4194816 | tf_op jit(solution)/shard_map/jit(_take)/gather | solution.py:57
  41.6 1.2 or_and_fusion
  42.8 3.7 %select_select_fusion = (bf16[128,64,128]{2,1,0:T(8,128)(2,1)}, bf16[128,64,128]{2,1,0:T(8,128)(2,1)}) fusion(bf16[128,64,128]{2,1,0:T(8,128)(2,1)S(1)} %gather_fusion.1, pred[128]{0:T(512)(128)(4,1)S(1)} %compare_and_fusion.2, pred[128]{0:T(512)(128)(4,1)S(1)} %and.166, bf16[128,64,128]{2,1,0:T(8,128)(2,1)} %gather_fusion), kind=kLoop, calls=%fused_computation.54 | loop fusion | flops 4194304 | bytes 8388864 | tf_op jit(solution)/shard_map/jit(_where)/select_n | solution.py:60
  46.6 84.0 %while.14 = (s32[]{:T(128)}, f32[24,8192]{1,0:T(8,128)S(1)}, f32[24,8192]{1,0:T(8,128)S(1)}, bf16[4,2,64,4,128]{4,3,2,1,0:T(4,128)(2,1)}, s32[4,32]{1,0:T(4,128)...) while((s32[]{:T(128)}, f32[24,8192]{1,0:T(8,128)S(1)}, ...), condition=%wide.region_9.11_spmd, body=%wide.region_3.10_spmd.sunk | while | flops 679871104 | bytes 52703944 | solution.py:110
  46.6 0.9 dynamic-slice_bitcast_fusion.6
  47.5 1.1 constant_dynamic-slice_fusion.4
  48.6 1.5 fusion.74
  50.9 1.3 copy-done
  52.2 1.7 %convolution_bitcast_fusion.5 = f32[2,1024,128]{2,1,0:T(8,128)} fusion(bf16[1,2,64,4,128]{4,3,2,1,0:T(4,128)(2,1)S(1)} %get-tuple-element.196, f32[2,4,64,1024]{3,2,1,0:T(8,128)S(1)} %get-tuple-element.194, f32[2,4,64]{2,1,0:T(4,128)S(1)} %get-tuple-element.195), kind=kOutput, calls=%fused_computation.16.clone.1 | convolution fusion | flops 135266304 | bytes 3278848 | tf_op jit(solution)/shard_map/while/body/eval_jaxpr/qgis,qigw->qsw/dot_general | solution.py:102
  53.9 1.4 reshape.340
  55.3 2.1 %scatter_fusion.1 = f32[24,8192]{1,0:T(8,128)S(1)} fusion(f32[24,8192]{1,0:T(8,128)S(1)} %get-tuple-element.212, s32[32]{0:T(128)S(1)} %fusion.73, f32[32,8192]{1,0:T(8,128)S(1)} %reshape.340), kind=kCustom, calls=%fused_computation.3.clone.1 | custom fusion | flops 262144 | bytes 3145856 | tf_op jit(solution)/shard_map/while/body/eval_jaxpr/scatter-add | solution.py:106
  57.4 2.4 %fusion.76 = (f32[2,4,64]{2,1,0:T(4,128)S(1)}, f32[2,1024,64,4]{1,2,3,0:T(8,128)S(1)}) fusion(f32[2,4,64,1024]{3,2,1,0:T(8,128)} %copy-done, f32[2,4,64]{2,1,0:T(4,128)S(1)} %get-tuple-element.195, bf16[1,2,64,4,128]{4,3,2,1,0:T(4,128)(2,1)S(1)} %get-tuple-element.196, bf16[4,2,1024,128]{3,2,1,0:T(8,128)(2,1)} %get-tuple-element.229, s32[]{:T(128)S(6)} %copy.84), kind=kOutput, calls=%fused_computation.7.clone.1 | convolution fusion | flops 135790080 | bytes 4853764 | tf_op jit(solution)/shard_map/while/body/eval_jaxpr/qigw,qsw->qgis/dot_general | solution.py:91
  60.2 1.5 fusion.79
  61.7 1.5 fusion.78
  63.3 1.4 reshape.339
  64.7 2.1 %scatter_fusion = f32[24,8192]{1,0:T(8,128)S(1)} fusion(f32[24,8192]{1,0:T(8,128)S(1)} %get-tuple-element.211, s32[32]{0:T(128)S(1)} %fusion.73, f32[32,8192]{1,0:T(8,128)S(1)} %reshape.339), kind=kCustom, calls=%fused_computation.2.clone.1 | custom fusion | flops 262144 | bytes 3145856 | tf_op jit(solution)/shard_map/while/body/eval_jaxpr/scatter-add | solution.py:105
  67.6 0.9 dynamic-slice_bitcast_fusion.6
  68.5 1.1 constant_dynamic-slice_fusion.4
  69.6 1.5 fusion.74
  71.9 1.3 copy-done
  73.2 1.7 %convolution_bitcast_fusion.5 = f32[2,1024,128]{2,1,0:T(8,128)} fusion(bf16[1,2,64,4,128]{4,3,2,1,0:T(4,128)(2,1)S(1)} %get-tuple-element.196, f32[2,4,64,1024]{3,2,1,0:T(8,128)S(1)} %get-tuple-element.194, f32[2,4,64]{2,1,0:T(4,128)S(1)} %get-tuple-element.195), kind=kOutput, calls=%fused_computation.16.clone.1 | convolution fusion | flops 135266304 | bytes 3278848 | tf_op jit(solution)/shard_map/while/body/eval_jaxpr/qgis,qigw->qsw/dot_general | solution.py:102
  74.9 1.4 reshape.340
  76.3 2.1 %scatter_fusion.1 = f32[24,8192]{1,0:T(8,128)S(1)} fusion(f32[24,8192]{1,0:T(8,128)S(1)} %get-tuple-element.212, s32[32]{0:T(128)S(1)} %fusion.73, f32[32,8192]{1,0:T(8,128)S(1)} %reshape.340), kind=kCustom, calls=%fused_computation.3.clone.1 | custom fusion | flops 262144 | bytes 3145856 | tf_op jit(solution)/shard_map/while/body/eval_jaxpr/scatter-add | solution.py:106
  78.4 2.4 %fusion.76 = (f32[2,4,64]{2,1,0:T(4,128)S(1)}, f32[2,1024,64,4]{1,2,3,0:T(8,128)S(1)}) fusion(f32[2,4,64,1024]{3,2,1,0:T(8,128)} %copy-done, f32[2,4,64]{2,1,0:T(4,128)S(1)} %get-tuple-element.195, bf16[1,2,64,4,128]{4,3,2,1,0:T(4,128)(2,1)S(1)} %get-tuple-element.196, bf16[4,2,1024,128]{3,2,1,0:T(8,128)(2,1)} %get-tuple-element.229, s32[]{:T(128)S(6)} %copy.84), kind=kOutput, calls=%fused_computation.7.clone.1 | convolution fusion | flops 135790080 | bytes 4853764 | tf_op jit(solution)/shard_map/while/body/eval_jaxpr/qigw,qsw->qgis/dot_general | solution.py:91
  81.2 1.5 fusion.79
  82.7 1.5 fusion.78
  84.3 1.4 reshape.339
  85.7 2.1 %scatter_fusion = f32[24,8192]{1,0:T(8,128)S(1)} fusion(f32[24,8192]{1,0:T(8,128)S(1)} %get-tuple-element.211, s32[32]{0:T(128)S(1)} %fusion.73, f32[32,8192]{1,0:T(8,128)S(1)} %reshape.339), kind=kCustom, calls=%fused_computation.2.clone.1 | custom fusion | flops 262144 | bytes 3145856 | tf_op jit(solution)/shard_map/while/body/eval_jaxpr/scatter-add | solution.py:105
  88.6 0.9 dynamic-slice_bitcast_fusion.6
  89.5 1.1 constant_dynamic-slice_fusion.4
  90.6 1.5 fusion.74
  92.9 1.3 copy-done
  94.2 1.7 %convolution_bitcast_fusion.5 = f32[2,1024,128]{2,1,0:T(8,128)} fusion(bf16[1,2,64,4,128]{4,3,2,1,0:T(4,128)(2,1)S(1)} %get-tuple-element.196, f32[2,4,64,1024]{3,2,1,0:T(8,128)S(1)} %get-tuple-element.194, f32[2,4,64]{2,1,0:T(4,128)S(1)} %get-tuple-element.195), kind=kOutput, calls=%fused_computation.16.clone.1 | convolution fusion | flops 135266304 | bytes 3278848 | tf_op jit(solution)/shard_map/while/body/eval_jaxpr/qgis,qigw->qsw/dot_general | solution.py:102
  95.9 1.4 reshape.340
  97.3 2.1 %scatter_fusion.1 = f32[24,8192]{1,0:T(8,128)S(1)} fusion(f32[24,8192]{1,0:T(8,128)S(1)} %get-tuple-element.212, s32[32]{0:T(128)S(1)} %fusion.73, f32[32,8192]{1,0:T(8,128)S(1)} %reshape.340), kind=kCustom, calls=%fused_computation.3.clone.1 | custom fusion | flops 262144 | bytes 3145856 | tf_op jit(solution)/shard_map/while/body/eval_jaxpr/scatter-add | solution.py:106
  99.4 2.4 %fusion.76 = (f32[2,4,64]{2,1,0:T(4,128)S(1)}, f32[2,1024,64,4]{1,2,3,0:T(8,128)S(1)}) fusion(f32[2,4,64,1024]{3,2,1,0:T(8,128)} %copy-done, f32[2,4,64]{2,1,0:T(4,128)S(1)} %get-tuple-element.195, bf16[1,2,64,4,128]{4,3,2,1,0:T(4,128)(2,1)S(1)} %get-tuple-element.196, bf16[4,2,1024,128]{3,2,1,0:T(8,128)(2,1)} %get-tuple-element.229, s32[]{:T(128)S(6)} %copy.84), kind=kOutput, calls=%fused_computation.7.clone.1 | convolution fusion | flops 135790080 | bytes 4853764 | tf_op jit(solution)/shard_map/while/body/eval_jaxpr/qigw,qsw->qgis/dot_general | solution.py:91
  102.2 1.5 fusion.79
  103.7 1.5 fusion.78
  105.3 1.4 reshape.339
  106.7 2.1 %scatter_fusion = f32[24,8192]{1,0:T(8,128)S(1)} fusion(f32[24,8192]{1,0:T(8,128)S(1)} %get-tuple-element.211, s32[32]{0:T(128)S(1)} %fusion.73, f32[32,8192]{1,0:T(8,128)S(1)} %reshape.339), kind=kCustom, calls=%fused_computation.2.clone.1 | custom fusion | flops 262144 | bytes 3145856 | tf_op jit(solution)/shard_map/while/body/eval_jaxpr/scatter-add | solution.py:105
  109.6 0.9 dynamic-slice_bitcast_fusion.6
  110.5 1.1 constant_dynamic-slice_fusion.4
  111.6 1.5 fusion.74
  113.9 1.3 copy-done
  115.2 1.7 %convolution_bitcast_fusion.5 = f32[2,1024,128]{2,1,0:T(8,128)} fusion(bf16[1,2,64,4,128]{4,3,2,1,0:T(4,128)(2,1)S(1)} %get-tuple-element.196, f32[2,4,64,1024]{3,2,1,0:T(8,128)S(1)} %get-tuple-element.194, f32[2,4,64]{2,1,0:T(4,128)S(1)} %get-tuple-element.195), kind=kOutput, calls=%fused_computation.16.clone.1 | convolution fusion | flops 135266304 | bytes 3278848 | tf_op jit(solution)/shard_map/while/body/eval_jaxpr/qgis,qigw->qsw/dot_general | solution.py:102
  116.9 1.4 reshape.340
  118.3 2.1 %scatter_fusion.1 = f32[24,8192]{1,0:T(8,128)S(1)} fusion(f32[24,8192]{1,0:T(8,128)S(1)} %get-tuple-element.212, s32[32]{0:T(128)S(1)} %fusion.73, f32[32,8192]{1,0:T(8,128)S(1)} %reshape.340), kind=kCustom, calls=%fused_computation.3.clone.1 | custom fusion | flops 262144 | bytes 3145856 | tf_op jit(solution)/shard_map/while/body/eval_jaxpr/scatter-add | solution.py:106
  120.4 2.4 %fusion.76 = (f32[2,4,64]{2,1,0:T(4,128)S(1)}, f32[2,1024,64,4]{1,2,3,0:T(8,128)S(1)}) fusion(f32[2,4,64,1024]{3,2,1,0:T(8,128)} %copy-done, f32[2,4,64]{2,1,0:T(4,128)S(1)} %get-tuple-element.195, bf16[1,2,64,4,128]{4,3,2,1,0:T(4,128)(2,1)S(1)} %get-tuple-element.196, bf16[4,2,1024,128]{3,2,1,0:T(8,128)(2,1)} %get-tuple-element.229, s32[]{:T(128)S(6)} %copy.84), kind=kOutput, calls=%fused_computation.7.clone.1 | convolution fusion | flops 135790080 | bytes 4853764 | tf_op jit(solution)/shard_map/while/body/eval_jaxpr/qigw,qsw->qgis/dot_general | solution.py:91
  123.2 1.5 fusion.79
  124.7 1.5 fusion.78
  126.3 1.4 reshape.339
  127.7 2.1 %scatter_fusion = f32[24,8192]{1,0:T(8,128)S(1)} fusion(f32[24,8192]{1,0:T(8,128)S(1)} %get-tuple-element.211, s32[32]{0:T(128)S(1)} %fusion.73, f32[32,8192]{1,0:T(8,128)S(1)} %reshape.339), kind=kCustom, calls=%fused_computation.2.clone.1 | custom fusion | flops 262144 | bytes 3145856 | tf_op jit(solution)/shard_map/while/body/eval_jaxpr/scatter-add | solution.py:105
  130.6 0.9 reshape.280
  131.5 4.1 %all-to-all-start = ((f32[4,4,8192]{2,1,0:T(4,128)}), f32[4,4,8192]{2,1,0:T(4,128)S(1)}, u32[]{:S(2)}, u32[]{:S(2)}) async-start(f32[4,4,8192]{2,1,0:T(4,128)} %reshape.280), calls=%async_computation | async-start | bytes 1048576 | tf_op jit(solution)/shard_map/all_to_all | solution.py:122
  136.1 1.0 reshape.282
  137.0 8.9 %all-to-all-done = f32[4,4,8192]{2,1,0:T(4,128)S(1)} async-done(((f32[4,4,8192]{2,1,0:T(4,128)}), f32[4,4,8192]{2,1,0:T(4,128)S(1)}, u32[]{:S(2)}, u32[]{:S(2)}) %all-to-all-start) | async-done | bytes 524320 | tf_op jit(solution)/shard_map/all_to_all | solution.py:122
  146.0 3.5 %all-to-all-start.1 = ((f32[4,4,8192]{2,1,0:T(4,128)}), f32[4,4,8192]{2,1,0:T(4,128)S(1)}, u32[]{:S(2)}, u32[]{:S(2)}) async-start(f32[4,4,8192]{2,1,0:T(4,128)} %reshape.282), calls=%async_computation.1 | async-start | bytes 1048576 | tf_op jit(solution)/shard_map/all_to_all | solution.py:123
  149.8 0.9 fusion.30
  150.7 9.0 %all-to-all-done.1 = f32[4,4,8192]{2,1,0:T(4,128)S(1)} async-done(((f32[4,4,8192]{2,1,0:T(4,128)}), f32[4,4,8192]{2,1,0:T(4,128)S(1)}, u32[]{:S(2)}, u32[]{:S(2)}) %all-to-all-start.1) | async-done | bytes 524320 | tf_op jit(solution)/shard_map/all_to_all | solution.py:123
  159.7 0.9 fusion.31
  160.6 4.8 %all-reduce.2 = (bf16[8,8192]{1,0:T(8,128)(2,1)S(1)}, bf16[8,8192]{1,0:T(8,128)(2,1)S(1)}) all-reduce(f32[8,8192]{1,0:T(8,128)S(1)} %fusion.30, f32[8,8192]{1,0:T(8,128)S(1)} %fusion.31), channel_id=1, replica_groups=mesh['groups'=2,'seq'=4,'head'=2,'inner'=2] {'inner'}, use_global_device_ids=true, to_apply=%region_12.14 | all-reduce | flops 131072 | bytes 786432 | tf_op jit(solution)/shard_map/psum | solution.py:131
  (77 shorter events, 14.0 us)
Async XLA Ops:
  50.9 1.3 copy-start
  57.4 2.4 %copy-start.1 = (f32[2,4,64,1024]{3,2,1,0:T(8,128)S(1)}, f32[2,4,64,1024]{3,2,1,0:T(8,128)}, u32[]{:S(2)}) copy-start(f32[2,4,64,1024]{3,2,1,0:T(8,128)} %copy-done) | copy-start | bytes 6291460 | tf_op jit(solution)/shard_map/while
  71.9 1.3 copy-start
  78.4 2.4 %copy-start.1 = (f32[2,4,64,1024]{3,2,1,0:T(8,128)S(1)}, f32[2,4,64,1024]{3,2,1,0:T(8,128)}, u32[]{:S(2)}) copy-start(f32[2,4,64,1024]{3,2,1,0:T(8,128)} %copy-done) | copy-start | bytes 6291460 | tf_op jit(solution)/shard_map/while
  92.9 1.3 copy-start
  99.4 2.4 %copy-start.1 = (f32[2,4,64,1024]{3,2,1,0:T(8,128)S(1)}, f32[2,4,64,1024]{3,2,1,0:T(8,128)}, u32[]{:S(2)}) copy-start(f32[2,4,64,1024]{3,2,1,0:T(8,128)} %copy-done) | copy-start | bytes 6291460 | tf_op jit(solution)/shard_map/while
  113.9 1.3 copy-start
  120.4 2.4 %copy-start.1 = (f32[2,4,64,1024]{3,2,1,0:T(8,128)S(1)}, f32[2,4,64,1024]{3,2,1,0:T(8,128)}, u32[]{:S(2)}) copy-start(f32[2,4,64,1024]{3,2,1,0:T(8,128)} %copy-done) | copy-start | bytes 6291460 | tf_op jit(solution)/shard_map/while
  131.5 14.4 %all-to-all-start = ((f32[4,4,8192]{2,1,0:T(4,128)}), f32[4,4,8192]{2,1,0:T(4,128)S(1)}, u32[]{:S(2)}, u32[]{:S(2)}) async-start(f32[4,4,8192]{2,1,0:T(4,128)} %reshape.280), calls=%async_computation | async-start | bytes 1048576 | tf_op jit(solution)/shard_map/all_to_all | solution.py:122
  146.0 13.7 %all-to-all-start.1 = ((f32[4,4,8192]{2,1,0:T(4,128)}), f32[4,4,8192]{2,1,0:T(4,128)S(1)}, u32[]{:S(2)}, u32[]{:S(2)}) async-start(f32[4,4,8192]{2,1,0:T(4,128)} %reshape.282), calls=%async_computation.1 | async-start | bytes 1048576 | tf_op jit(solution)/shard_map/all_to_all | solution.py:123
where the time goes:
time: 168 us; the launch traced here: 167 us
  blocking collectives  39 us (23%)
  local copies, waits for them, and re-layouts  37.2 us (22%)
  matrix products  36.2 us (22%)
  other arithmetic  27.9 us (17%)
  waiting for transfers between devices  17.9 us (11%)
  starting transfers between devices  7.61 us (5%)
    all_gather x1, blocking collectives, per_device(): key_piece = lax.all_gather(keys, 'seq', axis=0, tiled=True)  17.6 us
    all_gather x1, blocking collectives, per_device(): value_piece = lax.all_gather(values, 'seq', axis=0, tiled=True)  16.6 us
    dot_general x4, matrix products, attend(): jnp.einsum('qigw,qsw->qgis', do_group, v_group, preferred_element_type=jn...  9.67 us
    all_to_all x1, waiting for transfers between devices, per_device(): lax.all_to_all(send_value_tiles, 'seq', split_axis=0, concat_axis=0, tile...  9 us
    all_to_all x1, waiting for transfers between devices, per_device(): lax.all_to_all(send_key_tiles, 'seq', split_axis=0, concat_axis=0, tiled=...  8.93 us
    scatter-add x4, other arithmetic, attend(): key_acc.at[rows_group].add(key_terms.reshape(group * TOPK, BLK * width))  8.42 us
    scatter-add x4, other arithmetic, attend(): value_acc.at[rows_group].add(value_terms.reshape(group * TOPK, BLK * width))  8.42 us
    dot_general x4, matrix products, attend(): jnp.einsum('qgis,qigw->qsw', probs_b, do_group, preferred_element_type=jn...  6.69 us
  transfers between devices with their start and end apart: 2, of which 2 were waited for; matrix products, arithmetic and copies ran while one was open for 2% of the time, Pallas kernels for 0%

commit v1 on v0

--- a/solution.py
+++ b/solution.py
@@ -49,7 +49,9 @@
     blank = jnp.zeros((blocks_here * TOPK, BLK, width), jnp.bfloat16)
     carry = (blank, blank)
     key_piece = lax.all_gather(keys, "seq", axis=0, tiled=True)
-    value_piece = lax.all_gather(values, "seq", axis=0, tiled=True)
+    value_piece = jnp.concatenate(
+        lax.all_to_all(jnp.stack([values] * lax.axis_size("seq")), "seq", 0, 0), axis=0
+    )
     count = key_piece.shape[0] // BLK
     relative = wanted
     inside = (relative >= 0) & (relative < count)

time: 168 us -> 164 us (0.976)
  blocking collectives: 39 us -> 26 us
  starting transfers between devices: 7.61 us -> 14.3 us
  local copies, waits for them, and re-layouts: 37.2 us -> 39 us
    all_gather x1 -> x0, blocking collectives: 16.6 us -> none  [per_device(): value_piece = lax.all_gather(values, 'seq', axis=0, tiled=True)]
    all_to_all x0 -> x1, starting transfers between devices: none -> 6.35 us  [per_device(): lax.all_to_all(jnp.stack([values] * lax.axis_size('seq')), 'seq', 0, 0)]
    all_gather x1, blocking collectives: 17.6 us -> 21.2 us  [per_device(): key_piece = lax.all_gather(keys, 'seq', axis=0, tiled=True)]
    another operation x0 -> x1, local copies, waits for them, and re-layouts: none -> 1.8 us  [per_device(): jnp.stack([values] * lax.axis_size('seq'))]
  transfers between devices with their start and end apart: 2 -> 3, of which waited for: 2 -> 2; matrix products, arithmetic and copies ran while one was open for 2% -> 5% of each run, Pallas kernels for 0% -> 0%
where the time goes in v1:
time: 164 us; the launch traced here: 163 us
  local copies, waits for them, and re-layouts  39 us (24%)
  matrix products  36.2 us (22%)
  other arithmetic  27.9 us (17%)
  blocking collectives  26 us (16%)
  waiting for transfers between devices  18.1 us (11%)
  starting transfers between devices  14.3 us (9%)
    all_gather x1, blocking collectives, per_device(): key_piece = lax.all_gather(keys, 'seq', axis=0, tiled=True)  21.2 us
    dot_general x4, matrix products, attend(): jnp.einsum('qigw,qsw->qgis', do_group, v_group, preferred_element_type=jn...  9.68 us
    all_to_all x1, waiting for transfers between devices, per_device(): lax.all_to_all(send_key_tiles, 'seq', split_axis=0, concat_axis=0, tiled=...  9.09 us
    all_to_all x1, waiting for transfers between devices, per_device(): lax.all_to_all(send_value_tiles, 'seq', split_axis=0, concat_axis=0, tile...  9 us
    scatter-add x4, other arithmetic, attend(): key_acc.at[rows_group].add(key_terms.reshape(group * TOPK, BLK * width))  8.42 us
    scatter-add x4, other arithmetic, attend(): value_acc.at[rows_group].add(value_terms.reshape(group * TOPK, BLK * width))  8.42 us
    dot_general x4, matrix products, attend(): jnp.einsum('qgis,qigw->qsw', probs_b, do_group, preferred_element_type=jn...  6.69 us
    all_to_all x1, starting transfers between devices, per_device(): lax.all_to_all(jnp.stack([values] * lax.axis_size('seq')), 'seq', 0, 0)  6.35 us
  transfers between devices with their start and end apart: 3, of which 2 were waited for; matrix products, arithmetic and copies ran while one was open for 5% of the time, Pallas kernels for 0%

profile of v1, /device:TPU:0, one launch (start us, length us, event | category | flops | bytes accessed | tf_op | source)
XLA Modules:
  0.0 162.5 jit_solution(13147437198305870882)
XLA Ops:
  0.6 1.8 %stack.2 = bf16[4,512,1,128]{3,1,2,0:T(8,128)(2,1)} broadcast(bf16[512,128]{1,0:T(8,128)(2,1)} %bitcast.137), dimensions={1,3} | broadcast | bytes 655360 | tf_op jit(solution)/shard_map/stack | solution.py:53
  2.4 6.3 %all-to-all-start = ((bf16[4,512,1,128]{3,1,2,0:T(8,128)(2,1)}), bf16[4,512,1,128]{3,1,2,0:T(8,128)(2,1)S(1)}, u32[]{:S(2)}, u32[]{:S(2)}) async-start(bf16[4,512,1,128]{3,1,2,0:T(8,128)(2,1)} %stack.2), calls=%async_computation | async-start | bytes 1048576 | tf_op jit(solution)/shard_map/all_to_all | solution.py:53
  12.5 21.2 %all_gather.3 = bf16[2048,1,128]{2,0,1:T(8,128)(2,1)S(1)} all-gather(bf16[512,1,128]{2,0,1:T(8,128)(2,1)S(1)} %copy-done.2), channel_id=1, replica_groups=mesh['groups'=2,'seq'=4,'head'=2,'inner'=2] {'seq'}, dimensions={0}, use_global_device_ids=true | all-gather | bytes 655360 | tf_op jit(solution)/shard_map/all_gather | solution.py:51
  33.6 0.9 gather_fusion
  34.6 1.2 or_and_fusion
  35.8 2.1 %gather_fusion.1 = bf16[128,64,128]{2,1,0:T(8,128)(2,1)} fusion(bf16[32,64,128]{2,1,0:T(8,128)(2,1)S(1)} %bitcast.132, s32[1024]{0:T(1024)S(1)} %pad_clamp_fusion), kind=kCustom, calls=%fused_computation.1.clone | custom fusion | bytes 4194816 | tf_op jit(solution)/shard_map/jit(_take)/gather | solution.py:60
  38.0 3.7 %select_select_fusion = (bf16[128,64,128]{2,1,0:T(8,128)(2,1)}, bf16[128,64,128]{2,1,0:T(8,128)(2,1)}) fusion(bf16[128,64,128]{2,1,0:T(8,128)(2,1)} %gather_fusion.1, pred[128]{0:T(512)(128)(4,1)S(1)} %compare_and_fusion.2, pred[128]{0:T(512)(128)(4,1)S(1)} %and.166, bf16[128,64,128]{2,1,0:T(8,128)(2,1)S(1)} %gather_fusion), kind=kLoop, calls=%fused_computation.54 | loop fusion | flops 4194304 | bytes 8388864 | tf_op jit(solution)/shard_map/jit(_where)/select_n | solution.py:62
  41.8 84.0 %while.14 = (s32[]{:T(128)}, f32[24,8192]{1,0:T(8,128)S(1)}, f32[24,8192]{1,0:T(8,128)S(1)}, bf16[4,2,64,4,128]{4,3,2,1,0:T(4,128)(2,1)}, s32[4,32]{1,0:T(4,128)...) while((s32[]{:T(128)}, f32[24,8192]{1,0:T(8,128)S(1)}, ...), condition=%wide.region_9.11_spmd, body=%wide.region_3.10_spmd.sunk | while | flops 679871104 | bytes 52703944 | solution.py:112
  41.8 0.9 dynamic-slice_bitcast_fusion.6
  42.7 1.1 constant_dynamic-slice_fusion.4
  43.8 1.5 fusion.74
  46.1 1.3 copy-done
  47.4 1.7 %convolution_bitcast_fusion.5 = f32[2,1024,128]{2,1,0:T(8,128)} fusion(bf16[1,2,64,4,128]{4,3,2,1,0:T(4,128)(2,1)S(1)} %get-tuple-element.196, f32[2,4,64,1024]{3,2,1,0:T(8,128)S(1)} %get-tuple-element.194, f32[2,4,64]{2,1,0:T(4,128)S(1)} %get-tuple-element.195), kind=kOutput, calls=%fused_computation.16.clone.1 | convolution fusion | flops 135266304 | bytes 3278848 | tf_op jit(solution)/shard_map/while/body/eval_jaxpr/qgis,qigw->qsw/dot_general | solution.py:104
  49.1 1.4 reshape.343
  50.5 2.1 %scatter_fusion.1 = f32[24,8192]{1,0:T(8,128)S(1)} fusion(f32[24,8192]{1,0:T(8,128)S(1)} %get-tuple-element.212, s32[32]{0:T(128)S(1)} %fusion.73, f32[32,8192]{1,0:T(8,128)S(1)} %reshape.343), kind=kCustom, calls=%fused_computation.3.clone.1 | custom fusion | flops 262144 | bytes 3145856 | tf_op jit(solution)/shard_map/while/body/eval_jaxpr/scatter-add | solution.py:108
  52.6 2.4 %fusion.76 = (f32[2,4,64]{2,1,0:T(4,128)S(1)}, f32[2,1024,64,4]{1,2,3,0:T(8,128)S(1)}) fusion(f32[2,4,64,1024]{3,2,1,0:T(8,128)} %copy-done, f32[2,4,64]{2,1,0:T(4,128)S(1)} %get-tuple-element.195, bf16[1,2,64,4,128]{4,3,2,1,0:T(4,128)(2,1)S(1)} %get-tuple-element.196, bf16[4,2,1024,128]{3,2,1,0:T(8,128)(2,1)} %get-tuple-element.229, s32[]{:T(128)S(6)} %copy.84), kind=kOutput, calls=%fused_computation.7.clone.1 | convolution fusion | flops 135790080 | bytes 4853764 | tf_op jit(solution)/shard_map/while/body/eval_jaxpr/qigw,qsw->qgis/dot_general | solution.py:93
  55.4 1.5 fusion.79
  56.9 1.5 fusion.78
  58.5 1.4 reshape.342
  59.9 2.1 %scatter_fusion = f32[24,8192]{1,0:T(8,128)S(1)} fusion(f32[24,8192]{1,0:T(8,128)S(1)} %get-tuple-element.211, s32[32]{0:T(128)S(1)} %fusion.73, f32[32,8192]{1,0:T(8,128)S(1)} %reshape.342), kind=kCustom, calls=%fused_computation.2.clone.1 | custom fusion | flops 262144 | bytes 3145856 | tf_op jit(solution)/shard_map/while/body/eval_jaxpr/scatter-add | solution.py:107
  62.8 0.9 dynamic-slice_bitcast_fusion.6
  63.7 1.1 constant_dynamic-slice_fusion.4
  64.8 1.5 fusion.74
  67.1 1.3 copy-done
  68.4 1.7 %convolution_bitcast_fusion.5 = f32[2,1024,128]{2,1,0:T(8,128)} fusion(bf16[1,2,64,4,128]{4,3,2,1,0:T(4,128)(2,1)S(1)} %get-tuple-element.196, f32[2,4,64,1024]{3,2,1,0:T(8,128)S(1)} %get-tuple-element.194, f32[2,4,64]{2,1,0:T(4,128)S(1)} %get-tuple-element.195), kind=kOutput, calls=%fused_computation.16.clone.1 | convolution fusion | flops 135266304 | bytes 3278848 | tf_op jit(solution)/shard_map/while/body/eval_jaxpr/qgis,qigw->qsw/dot_general | solution.py:104
  70.1 1.4 reshape.343
  71.5 2.1 %scatter_fusion.1 = f32[24,8192]{1,0:T(8,128)S(1)} fusion(f32[24,8192]{1,0:T(8,128)S(1)} %get-tuple-element.212, s32[32]{0:T(128)S(1)} %fusion.73, f32[32,8192]{1,0:T(8,128)S(1)} %reshape.343), kind=kCustom, calls=%fused_computation.3.clone.1 | custom fusion | flops 262144 | bytes 3145856 | tf_op jit(solution)/shard_map/while/body/eval_jaxpr/scatter-add | solution.py:108
  73.6 2.4 %fusion.76 = (f32[2,4,64]{2,1,0:T(4,128)S(1)}, f32[2,1024,64,4]{1,2,3,0:T(8,128)S(1)}) fusion(f32[2,4,64,1024]{3,2,1,0:T(8,128)} %copy-done, f32[2,4,64]{2,1,0:T(4,128)S(1)} %get-tuple-element.195, bf16[1,2,64,4,128]{4,3,2,1,0:T(4,128)(2,1)S(1)} %get-tuple-element.196, bf16[4,2,1024,128]{3,2,1,0:T(8,128)(2,1)} %get-tuple-element.229, s32[]{:T(128)S(6)} %copy.84), kind=kOutput, calls=%fused_computation.7.clone.1 | convolution fusion | flops 135790080 | bytes 4853764 | tf_op jit(solution)/shard_map/while/body/eval_jaxpr/qigw,qsw->qgis/dot_general | solution.py:93
  76.4 1.5 fusion.79
  77.9 1.5 fusion.78
  79.5 1.4 reshape.342
  80.9 2.1 %scatter_fusion = f32[24,8192]{1,0:T(8,128)S(1)} fusion(f32[24,8192]{1,0:T(8,128)S(1)} %get-tuple-element.211, s32[32]{0:T(128)S(1)} %fusion.73, f32[32,8192]{1,0:T(8,128)S(1)} %reshape.342), kind=kCustom, calls=%fused_computation.2.clone.1 | custom fusion | flops 262144 | bytes 3145856 | tf_op jit(solution)/shard_map/while/body/eval_jaxpr/scatter-add | solution.py:107
  83.8 0.9 dynamic-slice_bitcast_fusion.6
  84.7 1.1 constant_dynamic-slice_fusion.4
  85.8 1.5 fusion.74
  88.1 1.3 copy-done
  89.4 1.7 %convolution_bitcast_fusion.5 = f32[2,1024,128]{2,1,0:T(8,128)} fusion(bf16[1,2,64,4,128]{4,3,2,1,0:T(4,128)(2,1)S(1)} %get-tuple-element.196, f32[2,4,64,1024]{3,2,1,0:T(8,128)S(1)} %get-tuple-element.194, f32[2,4,64]{2,1,0:T(4,128)S(1)} %get-tuple-element.195), kind=kOutput, calls=%fused_computation.16.clone.1 | convolution fusion | flops 135266304 | bytes 3278848 | tf_op jit(solution)/shard_map/while/body/eval_jaxpr/qgis,qigw->qsw/dot_general | solution.py:104
  91.1 1.4 reshape.343
  92.5 2.1 %scatter_fusion.1 = f32[24,8192]{1,0:T(8,128)S(1)} fusion(f32[24,8192]{1,0:T(8,128)S(1)} %get-tuple-element.212, s32[32]{0:T(128)S(1)} %fusion.73, f32[32,8192]{1,0:T(8,128)S(1)} %reshape.343), kind=kCustom, calls=%fused_computation.3.clone.1 | custom fusion | flops 262144 | bytes 3145856 | tf_op jit(solution)/shard_map/while/body/eval_jaxpr/scatter-add | solution.py:108
  94.6 2.4 %fusion.76 = (f32[2,4,64]{2,1,0:T(4,128)S(1)}, f32[2,1024,64,4]{1,2,3,0:T(8,128)S(1)}) fusion(f32[2,4,64,1024]{3,2,1,0:T(8,128)} %copy-done, f32[2,4,64]{2,1,0:T(4,128)S(1)} %get-tuple-element.195, bf16[1,2,64,4,128]{4,3,2,1,0:T(4,128)(2,1)S(1)} %get-tuple-element.196, bf16[4,2,1024,128]{3,2,1,0:T(8,128)(2,1)} %get-tuple-element.229, s32[]{:T(128)S(6)} %copy.84), kind=kOutput, calls=%fused_computation.7.clone.1 | convolution fusion | flops 135790080 | bytes 4853764 | tf_op jit(solution)/shard_map/while/body/eval_jaxpr/qigw,qsw->qgis/dot_general | solution.py:93
  97.4 1.5 fusion.79
  98.9 1.5 fusion.78
  100.5 1.4 reshape.342
  101.9 2.1 %scatter_fusion = f32[24,8192]{1,0:T(8,128)S(1)} fusion(f32[24,8192]{1,0:T(8,128)S(1)} %get-tuple-element.211, s32[32]{0:T(128)S(1)} %fusion.73, f32[32,8192]{1,0:T(8,128)S(1)} %reshape.342), kind=kCustom, calls=%fused_computation.2.clone.1 | custom fusion | flops 262144 | bytes 3145856 | tf_op jit(solution)/shard_map/while/body/eval_jaxpr/scatter-add | solution.py:107
  104.8 0.9 dynamic-slice_bitcast_fusion.6
  105.7 1.1 constant_dynamic-slice_fusion.4
  106.8 1.5 fusion.74
  109.1 1.3 copy-done
  110.4 1.7 %convolution_bitcast_fusion.5 = f32[2,1024,128]{2,1,0:T(8,128)} fusion(bf16[1,2,64,4,128]{4,3,2,1,0:T(4,128)(2,1)S(1)} %get-tuple-element.196, f32[2,4,64,1024]{3,2,1,0:T(8,128)S(1)} %get-tuple-element.194, f32[2,4,64]{2,1,0:T(4,128)S(1)} %get-tuple-element.195), kind=kOutput, calls=%fused_computation.16.clone.1 | convolution fusion | flops 135266304 | bytes 3278848 | tf_op jit(solution)/shard_map/while/body/eval_jaxpr/qgis,qigw->qsw/dot_general | solution.py:104
  112.1 1.4 reshape.343
  113.5 2.1 %scatter_fusion.1 = f32[24,8192]{1,0:T(8,128)S(1)} fusion(f32[24,8192]{1,0:T(8,128)S(1)} %get-tuple-element.212, s32[32]{0:T(128)S(1)} %fusion.73, f32[32,8192]{1,0:T(8,128)S(1)} %reshape.343), kind=kCustom, calls=%fused_computation.3.clone.1 | custom fusion | flops 262144 | bytes 3145856 | tf_op jit(solution)/shard_map/while/body/eval_jaxpr/scatter-add | solution.py:108
  115.6 2.4 %fusion.76 = (f32[2,4,64]{2,1,0:T(4,128)S(1)}, f32[2,1024,64,4]{1,2,3,0:T(8,128)S(1)}) fusion(f32[2,4,64,1024]{3,2,1,0:T(8,128)} %copy-done, f32[2,4,64]{2,1,0:T(4,128)S(1)} %get-tuple-element.195, bf16[1,2,64,4,128]{4,3,2,1,0:T(4,128)(2,1)S(1)} %get-tuple-element.196, bf16[4,2,1024,128]{3,2,1,0:T(8,128)(2,1)} %get-tuple-element.229, s32[]{:T(128)S(6)} %copy.84), kind=kOutput, calls=%fused_computation.7.clone.1 | convolution fusion | flops 135790080 | bytes 4853764 | tf_op jit(solution)/shard_map/while/body/eval_jaxpr/qigw,qsw->qgis/dot_general | solution.py:93
  118.4 1.5 fusion.79
  119.9 1.5 fusion.78
  121.5 1.4 reshape.342
  122.9 2.1 %scatter_fusion = f32[24,8192]{1,0:T(8,128)S(1)} fusion(f32[24,8192]{1,0:T(8,128)S(1)} %get-tuple-element.211, s32[32]{0:T(128)S(1)} %fusion.73, f32[32,8192]{1,0:T(8,128)S(1)} %reshape.342), kind=kCustom, calls=%fused_computation.2.clone.1 | custom fusion | flops 262144 | bytes 3145856 | tf_op jit(solution)/shard_map/while/body/eval_jaxpr/scatter-add | solution.py:107
  125.8 0.9 reshape.283
  126.7 4.4 %all-to-all-start.1 = ((f32[4,4,8192]{2,1,0:T(4,128)}), f32[4,4,8192]{2,1,0:T(4,128)S(1)}, u32[]{:S(2)}, u32[]{:S(2)}) async-start(f32[4,4,8192]{2,1,0:T(4,128)} %reshape.283), calls=%async_computation.1 | async-start | bytes 1048576 | tf_op jit(solution)/shard_map/all_to_all | solution.py:124
  131.6 1.0 reshape.285
  132.5 9.1 %all-to-all-done.1 = f32[4,4,8192]{2,1,0:T(4,128)S(1)} async-done(((f32[4,4,8192]{2,1,0:T(4,128)}), f32[4,4,8192]{2,1,0:T(4,128)S(1)}, u32[]{:S(2)}, u32[]{:S(2)}) %all-to-all-start.1) | async-done | bytes 524320 | tf_op jit(solution)/shard_map/all_to_all | solution.py:124
  141.6 3.5 %all-to-all-start.2 = ((f32[4,4,8192]{2,1,0:T(4,128)}), f32[4,4,8192]{2,1,0:T(4,128)S(1)}, u32[]{:S(2)}, u32[]{:S(2)}) async-start(f32[4,4,8192]{2,1,0:T(4,128)} %reshape.285), calls=%async_computation.2 | async-start | bytes 1048576 | tf_op jit(solution)/shard_map/all_to_all | solution.py:125
  145.5 0.9 fusion.30
  146.4 9.0 %all-to-all-done.2 = f32[4,4,8192]{2,1,0:T(4,128)S(1)} async-done(((f32[4,4,8192]{2,1,0:T(4,128)}), f32[4,4,8192]{2,1,0:T(4,128)S(1)}, u32[]{:S(2)}, u32[]{:S(2)}) %all-to-all-start.2) | async-done | bytes 524320 | tf_op jit(solution)/shard_map/all_to_all | solution.py:125
  156.2 4.8 %all-reduce.2 = (bf16[8,8192]{1,0:T(8,128)(2,1)S(1)}, bf16[8,8192]{1,0:T(8,128)(2,1)S(1)}) all-reduce(f32[8,8192]{1,0:T(8,128)S(1)} %fusion.30, f32[8,8192]{1,0:T(8,128)S(1)} %fusion.31), channel_id=1, replica_groups=mesh['groups'=2,'seq'=4,'head'=2,'inner'=2] {'inner'}, use_global_device_ids=true, to_apply=%region_12.14 | all-reduce | flops 131072 | bytes 786432 | tf_op jit(solution)/shard_map/psum | solution.py:133
  (81 shorter events, 14.8 us)
Async XLA Ops:
  0.6 11.8 %copy-start.2 = (bf16[512,1,128]{2,0,1:T(8,128)(2,1)S(1)}, bf16[512,1,128]{2,0,1:T(8,128)(2,1)}, u32[]{:S(2)}) copy-start(bf16[512,1,128]{2,0,1:T(8,128)(2,1)} %param.12) | copy-start | bytes 393220
  2.4 33.4 %all-to-all-start = ((bf16[4,512,1,128]{3,1,2,0:T(8,128)(2,1)}), bf16[4,512,1,128]{3,1,2,0:T(8,128)(2,1)S(1)}, u32[]{:S(2)}, u32[]{:S(2)}) async-start(bf16[4,512,1,128]{3,1,2,0:T(8,128)(2,1)} %stack.2), calls=%async_computation | async-start | bytes 1048576 | tf_op jit(solution)/shard_map/all_to_all | solution.py:53
  46.1 1.3 copy-start
  52.6 2.4 %copy-start.1 = (f32[2,4,64,1024]{3,2,1,0:T(8,128)S(1)}, f32[2,4,64,1024]{3,2,1,0:T(8,128)}, u32[]{:S(2)}) copy-start(f32[2,4,64,1024]{3,2,1,0:T(8,128)} %copy-done) | copy-start | bytes 6291460 | tf_op jit(solution)/shard_map/while
  67.1 1.3 copy-start
  73.6 2.4 %copy-start.1 = (f32[2,4,64,1024]{3,2,1,0:T(8,128)S(1)}, f32[2,4,64,1024]{3,2,1,0:T(8,128)}, u32[]{:S(2)}) copy-start(f32[2,4,64,1024]{3,2,1,0:T(8,128)} %copy-done) | copy-start | bytes 6291460 | tf_op jit(solution)/shard_map/while
  88.1 1.3 copy-start
  94.6 2.4 %copy-start.1 = (f32[2,4,64,1024]{3,2,1,0:T(8,128)S(1)}, f32[2,4,64,1024]{3,2,1,0:T(8,128)}, u32[]{:S(2)}) copy-start(f32[2,4,64,1024]{3,2,1,0:T(8,128)} %copy-done) | copy-start | bytes 6291460 | tf_op jit(solution)/shard_map/while
  109.1 1.3 copy-start
  115.6 2.4 %copy-start.1 = (f32[2,4,64,1024]{3,2,1,0:T(8,128)S(1)}, f32[2,4,64,1024]{3,2,1,0:T(8,128)}, u32[]{:S(2)}) copy-start(f32[2,4,64,1024]{3,2,1,0:T(8,128)} %copy-done) | copy-start | bytes 6291460 | tf_op jit(solution)/shard_map/while
  126.7 14.9 %all-to-all-start.1 = ((f32[4,4,8192]{2,1,0:T(4,128)}), f32[4,4,8192]{2,1,0:T(4,128)S(1)}, u32[]{:S(2)}, u32[]{:S(2)}) async-start(f32[4,4,8192]{2,1,0:T(4,128)} %reshape.283), calls=%async_computation.1 | async-start | bytes 1048576 | tf_op jit(solution)/shard_map/all_to_all | solution.py:124
  141.6 13.7 %all-to-all-start.2 = ((f32[4,4,8192]{2,1,0:T(4,128)}), f32[4,4,8192]{2,1,0:T(4,128)S(1)}, u32[]{:S(2)}, u32[]{:S(2)}) async-start(f32[4,4,8192]{2,1,0:T(4,128)} %reshape.285), calls=%async_computation.2 | async-start | bytes 1048576 | tf_op jit(solution)/shard_map/all_to_all | solution.py:125
